TPU v7x, 8 devices: a whole 2x2x1 slice. The times are simulated.
8 devices in a mesh: dp: 2 (over z, y), tp: 4 (over x, core).
Axes of the slice: x: 2, y: 2, z: 1, core: 2. Of those that a mesh axis runs over, the one named last changes fastest.
Arguments:
- x: bfloat16 [640, 3072], P('dp'), parts along dimension 0
- lengths: int32 [130], P('dp'), parts along dimension 0
- attn_gain: bfloat16 [2, 3072], replicated
- w_q: bfloat16 [2, 3072, 3072], P(None, None, 'tp')
- w_k: bfloat16 [2, 3072, 1024], P(None, None, 'tp')
- w_v: bfloat16 [2, 3072, 1024], P(None, None, 'tp')
- w_o: bfloat16 [2, 3072, 3072], P(None, 'tp')
- mlp_gain: bfloat16 [2, 3072], replicated
- w_gate: bfloat16 [2, 3072, 8192], P(None, None, 'tp')
- w_up: bfloat16 [2, 3072, 8192], P(None, None, 'tp')
- w_down: bfloat16 [2, 8192, 3072], P(None, 'tp')
- k_cache: bfloat16 [2, 130, 8, 1024, 128], P(None, 'dp', 'tp'), parts along dimension 1
- v_cache: bfloat16 [2, 130, 8, 1024, 128], P(None, 'dp', 'tp'), parts along dimension 1
Outputs:
- output: bfloat16 [640, 3072], P('dp'), parts along dimension 0
There are 2 independent parts. A program takes and returns all parts, laid end to end along the dimension named above; an argument that names none is the same for every part.
All inputs are finite; a program needn't handle non-finite values.
Results may differ from a plain program's by a relative error of at most 0.0197503.
Values are sent between devices in bfloat16 or wider.
A program may use at most 1 GiB of HBM per device.

v0:
```python
import jax
import jax.numpy as jnp
from jax import lax
from jax.sharding import PartitionSpec as P

ROPE_BASE = 500000.0
EPSILON = 1e-5


def rms_norm(x, norm_gain):
    x_f32 = x.astype(jnp.float32)
    inv_rms = lax.rsqrt(jnp.mean(x_f32 * x_f32, axis=-1, keepdims=True) + EPSILON)
    return (x_f32 * inv_rms * norm_gain.astype(jnp.float32)).astype(jnp.bfloat16)


def rope_tables(positions, head_dim):
    freq_exps = jnp.arange(0, head_dim, 2, dtype=jnp.float32) / head_dim
    angles = positions.astype(jnp.float32)[:, None] * jnp.power(ROPE_BASE, -freq_exps)[None, :]
    return jnp.cos(angles)[:, None, :], jnp.sin(angles)[:, None, :]


def apply_rope(vectors, cos_tab, sin_tab):
    half_dim = vectors.shape[-1] // 2
    vec_f32 = vectors.astype(jnp.float32)
    first = vec_f32[..., :half_dim]
    second = vec_f32[..., half_dim:]
    return jnp.concatenate([first * cos_tab - second * sin_tab, second * cos_tab + first * sin_tab], axis=-1).astype(jnp.bfloat16)


def project(normed, weight, head_dim):
    return jnp.dot(normed, weight, preferred_element_type=jnp.float32).astype(jnp.bfloat16).reshape(normed.shape[0], -1, head_dim)


def attention(q_rot, k_rot, v_new, k_cache, v_cache, lengths):
    dec_rows = lengths.shape[0] - 1
    kv_local = k_cache.shape[1]
    seq_len = k_cache.shape[2]
    head_dim = k_cache.shape[3]
    tok_count = q_rot.shape[0]
    chunk_len = tok_count - dec_rows
    attn_scale = head_dim ** -0.5
    q_grouped = q_rot.reshape(tok_count, kv_local, -1, head_dim)
    q_dec = q_grouped[:dec_rows]
    q_chk = q_grouped[dec_rows:]
    seq_ids = jnp.arange(seq_len)
    dec_cache = jnp.einsum('bgrd,bgsd->bgrs', q_dec, k_cache[:dec_rows], preferred_element_type=jnp.float32) * attn_scale
    dec_cache = jnp.where(seq_ids[None, None, None, :] < lengths[:dec_rows, None, None, None], dec_cache, -jnp.inf)
    dec_self = jnp.einsum('bgrd,bgd->bgr', q_dec, k_rot[:dec_rows], preferred_element_type=jnp.float32)[..., None] * attn_scale
    dec_prob = jax.nn.softmax(jnp.concatenate([dec_cache, dec_self], axis=-1), axis=-1).astype(jnp.bfloat16)
    dec_out = jnp.einsum('bgrs,bgsd->bgrd', dec_prob[..., :seq_len], v_cache[:dec_rows], preferred_element_type=jnp.float32) + dec_prob[..., seq_len:].astype(jnp.float32) * v_new[:dec_rows, :, None, :].astype(jnp.float32)
    chk_cache = jnp.einsum('cgrd,gsd->cgrs', q_chk, k_cache[dec_rows], preferred_element_type=jnp.float32) * attn_scale
    chk_cache = jnp.where(seq_ids[None, None, None, :] < lengths[dec_rows], chk_cache, -jnp.inf)
    chk_self = jnp.einsum('cgrd,jgd->cgrj', q_chk, k_rot[dec_rows:], preferred_element_type=jnp.float32) * attn_scale
    tok_ids = jnp.arange(chunk_len)
    causal_mask = tok_ids[None, :] <= tok_ids[:, None]
    chk_self = jnp.where(causal_mask[:, None, None, :], chk_self, -jnp.inf)
    chk_prob = jax.nn.softmax(jnp.concatenate([chk_cache, chk_self], axis=-1), axis=-1).astype(jnp.bfloat16)
    chk_out = jnp.einsum('cgrs,gsd->cgrd', chk_prob[..., :seq_len], v_cache[dec_rows], preferred_element_type=jnp.float32) + jnp.einsum('cgrj,jgd->cgrd', chk_prob[..., seq_len:], v_new[dec_rows:], preferred_element_type=jnp.float32)
    return jnp.concatenate([dec_out.reshape(dec_rows, -1), chk_out.reshape(chunk_len, -1)], axis=0).astype(jnp.bfloat16)


def decoder_layer(x, cos_tab, sin_tab, lengths, attn_gain, w_q, w_k, w_v, w_o, mlp_gain, w_gate, w_up, w_down, k_cache, v_cache):
    head_dim = k_cache.shape[-1]
    normed = rms_norm(x, attn_gain)
    q_rot = apply_rope(project(normed, w_q, head_dim), cos_tab, sin_tab)
    k_rot = apply_rope(project(normed, w_k, head_dim), cos_tab, sin_tab)
    v_new = project(normed, w_v, head_dim)
    attended = attention(q_rot, k_rot, v_new, k_cache, v_cache, lengths)
    attn_part = jnp.dot(attended, w_o, preferred_element_type=jnp.float32).astype(jnp.bfloat16)
    attn_sum = lax.psum(attn_part, 'tp')
    hidden = (x.astype(jnp.float32) + attn_sum.astype(jnp.float32)).astype(jnp.bfloat16)
    mlp_in = rms_norm(hidden, mlp_gain)
    gate_proj = jnp.dot(mlp_in, w_gate, preferred_element_type=jnp.float32)
    up_proj = jnp.dot(mlp_in, w_up, preferred_element_type=jnp.float32)
    activated = (jax.nn.silu(gate_proj) * up_proj).astype(jnp.bfloat16)
    mlp_part = jnp.dot(activated, w_down, preferred_element_type=jnp.float32).astype(jnp.bfloat16)
    mlp_sum = lax.psum(mlp_part, 'tp')
    return (hidden.astype(jnp.float32) + mlp_sum.astype(jnp.float32)).astype(jnp.bfloat16)


def solution(mesh):
    col_spec = P(None, None, 'tp')
    row_spec = P(None, 'tp', None)
    cache_spec = P(None, 'dp', 'tp', None, None)
    in_specs = (P('dp', None), P('dp'), P(), col_spec, col_spec, col_spec, row_spec, P(), col_spec, col_spec, row_spec, cache_spec, cache_spec)

    def body(x, lengths, attn_gain, w_q, w_k, w_v, w_o, mlp_gain, w_gate, w_up, w_down, k_cache, v_cache):
        dec_rows = lengths.shape[0] - 1
        chunk_len = x.shape[0] - dec_rows
        positions = jnp.concatenate([lengths[:dec_rows], lengths[dec_rows] + jnp.arange(chunk_len, dtype=jnp.int32)])
        cos_tab, sin_tab = rope_tables(positions, k_cache.shape[-1])
        hidden = x
        for layer_idx in range(w_q.shape[0]):
            hidden = decoder_layer(hidden, cos_tab, sin_tab, lengths, attn_gain[layer_idx], w_q[layer_idx], w_k[layer_idx], w_v[layer_idx], w_o[layer_idx], mlp_gain[layer_idx], w_gate[layer_idx], w_up[layer_idx], w_down[layer_idx], k_cache[layer_idx], v_cache[layer_idx])
        return hidden

    return jax.shard_map(body, mesh=mesh, in_specs=in_specs, out_specs=P('dp', None), check_vma=False)
```

profile of v0, /device:TPU:0, one launch (start us, length us, event | category | flops | bytes accessed | tf_op | source)
XLA Modules:
  0.0 452.2 jit_solution(6760817025370214711)
XLA Ops:
  13.2 2.9 fusion.132
  19.6 5.0 %fusion.115 = f32[320,768]{1,0:T(8,128)} fusion(bf16[2,3072,768]{2,1,0:T(8,128)(2,1)} %param.16, bf16[320,3072]{1,0:T(8,128)(2,1)S(1)} %copy-done.5, f32[3072]{0:T(1024)S(1)} %bitcast.263, f32[320]{0:T(512)S(1)} %add_rsqrt_fusion.3), kind=kOutput, calls=%fused_computation.121 | convolution fusion | flops 1514373120 | bytes 7681280 | tf_op jit(solution)/shard_map/dot_general | solution.py:31
  31.4 14.3 %fusion.6 = f32[64,2,3,1024]{3,2,1,0:T(4,128)S(1)} fusion(bf16[64,2,3,128]{3,2,1,0:T(4,128)(2,1)} %copy-done.24, bf16[2,65,2,1024,128]{4,3,2,1,0:T(8,128)(2,1)} %param.24), kind=kOutput, calls=%fused_computation.6 | convolution fusion | flops 100663296 | bytes 35258368 | tf_op jit(solution)/shard_map/bgrd,bgsd->bgrs/dot_general | solution.py:46
  45.7 4.3 copy.118
  50.0 4.7 %fusion.210 = (f32[64,2,3]{0,1,2:T(2,128)S(1)}, f32[64,2,3,1024]{0,1,3,2:T(2,128)S(1)}) fusion(f32[64,2,3,1024]{0,1,3,2:T(2,128)} %copy.118, pred[64,1024]{0,1:T(8,128)(4,1)} %iota_compare_fusion), kind=kLoop, calls=%fused_computation.211 | loop fusion | flops 1179264 | bytes 3212800 | tf_op jit(solution)/shard_map/reduce_max | solution.py:49
  59.4 5.9 %fusion.203 = f32[64,2,3]{0,1,2:T(2,128)S(1)} fusion(f32[64,2,3]{0,1,2:T(2,128)} %copy.125, f32[64,2,3,1]{0,1,3,2:T(2,128)S(1)} %bitcast.256, f32[64,2,3,1024]{0,1,3,2:T(2,128)S(1)} %get-tuple-element.12), kind=kLoop, calls=%fused_computation.209 | loop fusion | flops 1180416 | bytes 1577472 | tf_op jit(solution)/shard_map/reduce_sum | solution.py:49
  65.4 4.8 %divide_convert_fusion.3 = bf16[64,2,3,1025]{0,1,3,2:T(2,128)(2,1)S(1)} fusion(f32[64,2,3]{0,1,2:T(2,128)S(1)} %fusion.203, f32[64,2,3]{0,1,2:T(2,128)S(1)} %copy-done.32, f32[64,2,3,1]{0,1,3,2:T(2,128)S(1)} %bitcast.257, f32[64,2,3,1024]{0,1,3,2:T(2,128)S(1)} %get-tuple-element.12), kind=kLoop, calls=%fused_computation.89 | loop fusion | flops 1574400 | bytes 2364672 | tf_op jit(solution)/shard_map/convert_element_type | solution.py:49
  73.5 13.6 %fusion.147 = bf16[64,2,3,128]{3,2,1,0:T(4,128)(2,1)S(1)} fusion(bf16[64,2,3,1024]{3,2,1,0:T(4,128)(2,1)S(1)} %copy.126, bf16[2,65,2,1024,128]{4,3,2,1,0:T(8,128)(2,1)} %param.25, f32[64,2,128]{2,1,0:T(2,128)S(1)} %reshape.244, f32[64,2,3]{2,1,0:T(2,128)S(1)} %copy.127), kind=kOutput, calls=%fused_computation.133 | convolution fusion | flops 100810752 | bytes 34506240 | tf_op jit(solution)/shard_map/bgrs,bgsd->bgrd/dot_general | solution.py:50
  95.9 3.1 fusion.46
  99.9 45.7 %all-reduce.5.cloned.1.call-done = bf16[320,3072]{1,0:T(8,128)(2,1)} async-done(((bf16[320,3072]{1,0:T(8,128)(2,1)}), bf16[320,3072]{1,0:T(8,128)(2,1)}) %all-reduce.5.cloned.1.call-update) | async-done | bytes 1966096 | tf_op jit(solution)/shard_map/psum | solution.py:70
  145.6 3.0 fusion.62
  148.7 10.3 %fusion.22 = f32[320,2048]{1,0:T(8,128)} fusion(bf16[2,3072,2048]{2,1,0:T(8,128)(2,1)} %param.21, bf16[320,3072]{1,0:T(8,128)(2,1)S(1)} %get-tuple-element.10, f32[3072]{0:T(1024)S(1)} %bitcast.265, f32[320]{0:T(512)S(1)} %add_rsqrt_fusion.2), kind=kOutput, calls=%fused_computation.22 | convolution fusion | flops 4030464000 | bytes 17184000 | tf_op jit(solution)/shard_map/dot_general | solution.py:73
  159.0 15.3 %fusion.52 = bf16[320,3072]{1,0:T(8,128)(2,1)} fusion(bf16[2,2048,3072]{2,1,0:T(8,128)(2,1)} %param.23, bf16[2,3072,2048]{2,1,0:T(8,128)(2,1)} %param.22, f32[320,2048]{1,0:T(8,128)} %fusion.22, bf16[320,3072]{1,0:T(8,128)(2,1)S(1)} %get-tuple-element.10, f32[3072]{0:T(1024)S(1)} %bitcast.266, f32[320]{0:T(512)S(1)} %add_rsqrt_fusion.2), kind=kOutput, calls=%fused_computation.66 | convolution fusion | flops 8061911040 | bytes 31732992 | tf_op jit(solution)/shard_map/dot_general | solution.py:76
  174.4 43.7 %all-reduce.7.cloned.1.call-done = bf16[320,3072]{1,0:T(8,128)(2,1)} async-done(((bf16[320,3072]{1,0:T(8,128)(2,1)}), bf16[320,3072]{1,0:T(8,128)(2,1)}) %all-reduce.7.cloned.1.call-update) | async-done | bytes 1966096 | tf_op jit(solution)/shard_map/psum | solution.py:77
  224.4 2.8 fusion.138
  227.3 2.6 fusion.121
  234.3 15.4 %fusion.2 = f32[64,2,3,1024]{3,2,1,0:T(4,128)} fusion(bf16[64,2,3,128]{3,2,1,0:T(4,128)(2,1)S(1)} %copy.135, bf16[2,65,2,1024,128]{4,3,2,1,0:T(8,128)(2,1)} %param.24), kind=kOutput, calls=%fused_computation.2 | convolution fusion | flops 100663296 | bytes 35225600 | tf_op jit(solution)/shard_map/bgrd,bgsd->bgrs/dot_general | solution.py:46
  250.9 6.4 %copy.136 = f32[64,2,3,1024]{0,1,3,2:T(2,128)} copy(f32[64,2,3,1024]{3,2,1,0:T(4,128)} %fusion.2) | data formatting | bytes 3145728 | tf_op jit(solution)/shard_map/bgrd,bgsd->bgrs/dot_general | solution.py:46
  257.3 6.3 %fusion.208 = (f32[64,2,3]{0,1,2:T(2,128)S(1)}, f32[64,2,3,1024]{0,1,3,2:T(2,128)}) fusion(f32[64,2,3,1024]{0,1,3,2:T(2,128)} %copy.136, pred[64,1024]{0,1:T(8,128)(4,1)S(1)} %copy-done.23), kind=kLoop, calls=%fused_computation.210 | loop fusion | flops 1179264 | bytes 3212800 | tf_op jit(solution)/shard_map/reduce_max | solution.py:49
  264.0 6.6 %fusion.202 = f32[64,2,3]{0,1,2:T(2,128)S(1)} fusion(f32[64,2,3]{0,1,2:T(2,128)S(1)} %copy.141, f32[64,2,3,1]{0,1,3,2:T(2,128)S(1)} %bitcast.258, f32[64,2,3,1024]{0,1,3,2:T(2,128)} %get-tuple-element.8), kind=kLoop, calls=%fused_computation.208 | loop fusion | flops 1180416 | bytes 1577472 | tf_op jit(solution)/shard_map/reduce_sum | solution.py:49
  270.6 4.8 %divide_convert_fusion.2 = bf16[64,2,3,1025]{0,1,3,2:T(2,128)(2,1)S(1)} fusion(f32[64,2,3]{0,1,2:T(2,128)S(1)} %fusion.202, f32[64,2,3]{0,1,2:T(2,128)S(1)} %copy.141, f32[64,2,3,1]{0,1,3,2:T(2,128)S(1)} %bitcast.259, f32[64,2,3,1024]{0,1,3,2:T(2,128)S(1)} %copy-done.1), kind=kLoop, calls=%fused_computation.88 | loop fusion | flops 1574400 | bytes 2364672 | tf_op jit(solution)/shard_map/convert_element_type | solution.py:49
  279.0 4.8 %fusion.215 = (f32[256,2,3]{0,2,1:T(4,128)S(1)}, f32[256,2,3,1024]{3,0,2,1:T(8,128)}) fusion(bf16[256,2,3,128]{0,3,2,1:T(8,128)(2,1)S(1)} %bitcast.244, bf16[2,65,2,1024,128]{4,3,2,1,0:T(8,128)(2,1)} %param.24, pred[1024]{0:T(1024)(128)(4,1)S(1)} %copy-done.34), kind=kOutput, calls=%fused_computation.216 | convolution fusion | flops 407370240 | bytes 7216128 | tf_op jit(solution)/shard_map/cgrd,gsd->cgrs/dot_general | solution.py:51
  286.9 6.1 %copy.142 = bf16[64,2,3,1024]{3,2,1,0:T(4,128)(2,1)} copy(bf16[64,2,3,1024]{0,1,3,2:T(2,128)(2,1)} %slice.300) | data formatting | bytes 1572864 | tf_op jit(solution)/shard_map/slice | solution.py:50
  294.5 14.4 %fusion.153 = bf16[64,2,3,128]{3,2,1,0:T(4,128)(2,1)} fusion(bf16[64,2,3,1024]{3,2,1,0:T(4,128)(2,1)} %copy.142, bf16[2,65,2,1024,128]{4,3,2,1,0:T(8,128)(2,1)} %param.25, f32[64,2,128]{2,1,0:T(2,128)} %reshape.250, f32[64,2,3]{2,1,0:T(2,128)} %copy.143), kind=kOutput, calls=%fused_computation.135 | convolution fusion | flops 100810752 | bytes 34832384 | tf_op jit(solution)/shard_map/bgrs,bgsd->bgrd/dot_general | solution.py:50
  310.6 3.8 fusion.32
  319.7 3.2 fusion.49
  323.0 43.7 %all-reduce.9.cloned.1.call-done = bf16[320,3072]{1,0:T(8,128)(2,1)} async-done(((bf16[320,3072]{1,0:T(8,128)(2,1)}), bf16[320,3072]{1,0:T(8,128)(2,1)}) %all-reduce.9.cloned.1.call-update) | async-done | bytes 1966096 | tf_op jit(solution)/shard_map/psum | solution.py:70
  366.7 3.3 fusion.70
  371.3 10.4 %fusion.16 = f32[320,2048]{1,0:T(8,128)} fusion(bf16[2,3072,2048]{2,1,0:T(8,128)(2,1)} %param.21, bf16[320,3072]{1,0:T(8,128)(2,1)S(1)} %get-tuple-element.6, f32[3072]{0:T(1024)S(1)} %bitcast.260, f32[320]{0:T(512)S(1)} %add_rsqrt_fusion), kind=kOutput, calls=%fused_computation.16 | convolution fusion | flops 4030464000 | bytes 17184000 | tf_op jit(solution)/shard_map/dot_general | solution.py:73
  381.7 16.5 %fusion.55 = bf16[320,3072]{1,0:T(8,128)(2,1)} fusion(bf16[2,2048,3072]{2,1,0:T(8,128)(2,1)} %param.23, bf16[2,3072,2048]{2,1,0:T(8,128)(2,1)} %param.22, f32[320,2048]{1,0:T(8,128)} %fusion.16, bf16[320,3072]{1,0:T(8,128)(2,1)} %copy-done.3, f32[3072]{0:T(1024)S(1)} %bitcast.261, f32[320]{0:T(512)S(1)} %add_rsqrt_fusion), kind=kOutput, calls=%fused_computation.67 | convolution fusion | flops 8061911040 | bytes 31732992 | tf_op jit(solution)/shard_map/dot_general | solution.py:76
  398.2 43.7 %all-reduce.11.cloned.1.call-done = bf16[320,3072]{1,0:T(8,128)(2,1)} async-done(((bf16[320,3072]{1,0:T(8,128)(2,1)}), bf16[320,3072]{1,0:T(8,128)(2,1)}) %all-reduce.11.cloned.1.call-update) | async-done | bytes 1966096 | tf_op jit(solution)/shard_map/psum | solution.py:77
  442.0 3.5 fusion.73
  (190 shorter events, 62.7 us)
Async XLA Ops:
  6.5 139.1 %all-reduce.5.cloned.1.call-start = ((), (), s32[]{:S(2)}) async-start(), calls=%async_computation | async-start | bytes 3932160 | tf_op jit(solution)/shard_map/psum | solution.py:70
  13.1 6.4 %copy-start.36 = (f32[1,3072]{1,0:T(1,128)}, f32[1,3072]{1,0:T(1,128)S(1)}, u32[]{:S(2)}) copy-start(f32[1,3072]{1,0:T(1,128)S(1)} %get-tuple-element.31) | copy-start | bytes 36868
  13.1 6.4 %copy-start.5 = (bf16[320,3072]{1,0:T(8,128)(2,1)S(1)}, bf16[320,3072]{1,0:T(8,128)(2,1)}, u32[]{:S(2)}) copy-start(bf16[320,3072]{1,0:T(8,128)(2,1)} %param.13) | copy-start | bytes 5898244
  18.0 8.2 %copy-start.7 = (f32[320,64]{0,1:T(8,128)}, f32[320,64]{0,1:T(8,128)S(1)}, u32[]{:S(2)}) copy-start(f32[320,64]{0,1:T(8,128)S(1)} %get-tuple-element.33) | copy-start | bytes 245764
  18.0 8.2 %copy-start.9 = (f32[320,64]{0,1:T(8,128)}, f32[320,64]{0,1:T(8,128)S(1)}, u32[]{:S(2)}) copy-start(f32[320,64]{0,1:T(8,128)S(1)} %get-tuple-element.34) | copy-start | bytes 245764
  59.4 5.9 %copy-start.32 = (f32[64,2,3]{0,1,2:T(2,128)S(1)}, f32[64,2,3]{0,1,2:T(2,128)}, u32[]{:S(2)}) copy-start(f32[64,2,3]{0,1,2:T(2,128)} %copy.125) | copy-start | bytes 4612
  73.4 13.8 %copy-start.12 = (bf16[320,2,64]{2,0,1:T(8,128)(2,1)S(1)}, bf16[320,2,64]{2,0,1:T(8,128)(2,1)}, u32[]{:S(2)}) copy-start(bf16[320,2,64]{2,0,1:T(8,128)(2,1)} %copy-done.11) | copy-start | bytes 245764
  73.5 13.8 %copy-start.14 = (bf16[320,2,64]{2,0,1:T(8,128)(2,1)S(1)}, bf16[320,2,64]{2,0,1:T(8,128)(2,1)}, u32[]{:S(2)}) copy-start(bf16[320,2,64]{2,0,1:T(8,128)(2,1)} %copy-done.13) | copy-start | bytes 245764
  73.5 13.8 %copy-start.25 = (pred[256,256]{1,0:T(8,128)(4,1)S(1)}, pred[256,256]{1,0:T(8,128)(4,1)}, u32[]{:S(2)}) copy-start(pred[256,256]{1,0:T(8,128)(4,1)} %iota_compare_fusion.1) | copy-start | bytes 196612
  73.5 14.5 %copy-start.33 = (pred[1024]{0:T(1024)(128)(4,1)S(1)}, pred[1024]{0:T(1024)(128)(4,1)}, u32[]{:S(2)}) copy-start(pred[1024]{0:T(1024)(128)(4,1)} %iota_compare_fusion.2) | copy-start | bytes 3076
  90.3 5.6 %slice-start.4 = ((s8[9437184]{0:T(1024)(128)(4,1)}), s8[4194304]{0:T(1024)(128)(4,1)S(1)}, s32[]{:S(2)}) async-start(s8[9437184]{0:T(1024)(128)(4,1)} %bitcast.271), calls=%async_computation.8 | async-start | bytes 8388608
  99.1 119.0 %all-reduce.7.cloned.1.call-start = ((), (), s32[]{:S(2)}) async-start(), calls=%async_computation.1 | async-start | bytes 3932160 | tf_op jit(solution)/shard_map/psum | solution.py:77
  174.3 192.4 %all-reduce.9.cloned.1.call-start = ((), (), s32[]{:S(2)}) async-start(), calls=%async_computation.2 | async-start | bytes 3932160 | tf_op jit(solution)/shard_map/psum | solution.py:70
  218.1 9.1 %slice-start.1 = ((s8[9437184]{0:T(1024)(128)(4,1)}), s8[4194304]{0:T(1024)(128)(4,1)S(1)}, s32[]{:S(2)}) async-start(s8[9437184]{0:T(1024)(128)(4,1)} %bitcast.269), calls=%async_computation.5 | async-start | bytes 8388608
  220.6 6.7 %slice-start.2 = ((s8[9437184]{0:T(1024)(128)(4,1)}), s8[4194304]{0:T(1024)(128)(4,1)S(1)}, s32[]{:S(2)}) async-start(s8[9437184]{0:T(1024)(128)(4,1)} %bitcast.269), calls=%async_computation.6 | async-start | bytes 8388608
  222.4 4.8 %slice-start.3 = ((s8[9437184]{0:T(1024)(128)(4,1)}), s8[1048576]{0:T(1024)(128)(4,1)S(1)}, s32[]{:S(2)}) async-start(s8[9437184]{0:T(1024)(128)(4,1)} %bitcast.269), calls=%async_computation.7 | async-start | bytes 2097152
  227.2 4.2 copy-start.8
  234.3 15.4 %copy-start.20 = (f32[320,64]{1,0:T(8,128)S(1)}, f32[320,64]{1,0:T(8,128)}, u32[]{:S(2)}) copy-start(f32[320,64]{1,0:T(8,128)} %copy.120) | copy-start | bytes 245764
  234.3 15.4 %copy-start.22 = (f32[320,64]{1,0:T(8,128)S(1)}, f32[320,64]{1,0:T(8,128)}, u32[]{:S(2)}) copy-start(f32[320,64]{1,0:T(8,128)} %copy.122) | copy-start | bytes 245764
  249.9 7.4 %copy-start.23 = (pred[64,1024]{0,1:T(8,128)(4,1)S(1)}, pred[64,1024]{0,1:T(8,128)(4,1)}, u32[]{:S(2)}) copy-start(pred[64,1024]{0,1:T(8,128)(4,1)} %iota_compare_fusion) | copy-start | bytes 196612
  264.0 6.6 %copy-start.1 = (f32[64,2,3,1024]{0,1,3,2:T(2,128)S(1)}, f32[64,2,3,1024]{0,1,3,2:T(2,128)}, u32[]{:S(2)}) copy-start(f32[64,2,3,1024]{0,1,3,2:T(2,128)} %get-tuple-element.8) | copy-start | bytes 4718596
  270.6 7.7 %copy-start.6 = (bf16[256,6,128]{0,2,1:T(8,128)(2,1)S(1)}, bf16[256,6,128]{0,2,1:T(8,128)(2,1)}, u32[]{:S(2)}) copy-start(bf16[256,6,128]{0,2,1:T(8,128)(2,1)} %pad_maximum_fusion) | copy-start | bytes 1179652
  270.6 7.7 %copy-start.16 = (bf16[320,2,64]{2,0,1:T(8,128)(2,1)S(1)}, bf16[320,2,64]{2,0,1:T(8,128)(2,1)}, u32[]{:S(2)}) copy-start(bf16[320,2,64]{2,0,1:T(8,128)(2,1)} %copy-done.15) | copy-start | bytes 245764
  270.6 7.7 %copy-start.18 = (bf16[320,2,64]{2,0,1:T(8,128)(2,1)S(1)}, bf16[320,2,64]{2,0,1:T(8,128)(2,1)}, u32[]{:S(2)}) copy-start(bf16[320,2,64]{2,0,1:T(8,128)(2,1)} %copy-done.17) | copy-start | bytes 245764
  270.6 7.7 %copy-start.26 = (pred[256,256]{1,0:T(8,128)(4,1)S(1)}, pred[256,256]{1,0:T(8,128)(4,1)}, u32[]{:S(2)}) copy-start(pred[256,256]{1,0:T(8,128)(4,1)} %iota_compare_fusion.1) | copy-start | bytes 196612
  310.6 4.6 %copy-start = (f32[256,2,3,1024]{3,0,2,1:T(8,128)S(1)}, f32[256,2,3,1024]{3,0,2,1:T(8,128)}, u32[]{:S(2)}) copy-start(f32[256,2,3,1024]{3,0,2,1:T(8,128)} %get-tuple-element.40) | copy-start | bytes 18874372
  310.6 9.1 %slice-start.7 = ((s8[9437184]{0:T(1024)(128)(4,1)}), s8[4194304]{0:T(1024)(128)(4,1)S(1)}, s32[]{:S(2)}) async-start(s8[9437184]{0:T(1024)(128)(4,1)} %bitcast.273), calls=%async_computation.11 | async-start | bytes 8388608
  315.3 4.4 slice-start.8
  315.3 4.4 slice-start.9
  323.0 48.3 %copy-start.35 = (f32[1,3072]{1,0:T(1,128)S(1)}, f32[1,3072]{1,0:T(1,128)}, u32[]{:S(2)}) copy-start(f32[1,3072]{1,0:T(1,128)} %get-tuple-element.29) | copy-start | bytes 36868
  323.0 119.0 %all-reduce.11.cloned.1.call-start = ((), (), s32[]{:S(2)}) async-start(), calls=%async_computation.3 | async-start | bytes 3932160 | tf_op jit(solution)/shard_map/psum | solution.py:77
  398.2 43.8 %copy-start.4 = (bf16[320,3072]{1,0:T(8,128)(2,1)S(1)}, bf16[320,3072]{1,0:T(8,128)(2,1)}, u32[]{:S(2)}) copy-start(bf16[320,3072]{1,0:T(8,128)(2,1)} %copy-done.3) | copy-start | bytes 5898244
  (23 other events, 47.2 us)
Sparse Core Ops, SparseCore 0:
  99.2 46.3 all-reduce.4
  174.5 43.5 all-reduce.6
  323.1 43.5 all-reduce.8
  398.3 43.5 all-reduce.10
where the time goes:
time: 458 us; the launch traced here: 452 us
  waiting for transfers between devices  177 us (39%)
  matrix products  147 us (32%)
  other arithmetic  67.1 us (15%)
  local copies, waits for them, and re-layouts  47.1 us (10%)
  between operations  14.2 us (3%)
    psum x2, waiting for transfers between devices, decoder_layer(): attn_sum = lax.psum(attn_part, 'tp')  89.4 us
    psum x2, waiting for transfers between devices, decoder_layer(): mlp_sum = lax.psum(mlp_part, 'tp')  87.5 us
    dot_general x2, matrix products, decoder_layer(): jnp.dot(activated, w_down, preferred_element_type=jnp.float32)  31.8 us
    dot_general x2, matrix products, attention(): jnp.einsum('bgrd,bgsd->bgrs', q_dec, k_cache[:dec_rows], preferred_elemen...  29.7 us
    dot_general x2, matrix products, attention(): jnp.einsum('bgrs,bgsd->bgrd', dec_prob[..., :seq_len], v_cache[:dec_rows]...  28 us
    dot_general x2, matrix products, decoder_layer(): gate_proj = jnp.dot(mlp_in, w_gate, preferred_element_type=jnp.float32)  20.7 us
    dot_general x6, matrix products, project(): jnp.dot(normed, weight, preferred_element_type=jnp.float32)  14.8 us
    reduce_sum x2, other arithmetic, attention(): jax.nn.softmax(jnp.concatenate([dec_cache, dec_self], axis=-1), axis=-1)  12.5 us
  transfers between devices with their start and end apart: 4, of which 4 were waited for; matrix products, arithmetic and copies ran while one was open for 0% of the time, Pallas kernels for 0%

commit v1 on v0

v1 whole, which is shorter than its diff:
```python
import functools

import jax
import jax.numpy as jnp
from jax import lax
from jax.experimental import pallas as pl
from jax.experimental.pallas import tpu as pltpu
from jax.sharding import PartitionSpec as P

ROPE_BASE = 500000.0
EPSILON = 1e-5
MESH = pl.DeviceIdType.MESH
F32 = jnp.float32
BF16 = jnp.bfloat16
VMEM_LIMIT = 66_900_000
TILE = 256
GROUPS = ((0, 160), (160, 160))


def rope_tables(positions, head_dim):
    freq_exps = jnp.arange(0, head_dim, 2, dtype=F32) / head_dim
    angles = positions.astype(F32)[:, None] * jnp.power(ROPE_BASE, -freq_exps)[None, :]
    cos_half, sin_half = jnp.cos(angles), jnp.sin(angles)
    return jnp.concatenate([cos_half, cos_half], axis=-1), jnp.concatenate([-sin_half, sin_half], axis=-1)


def norm_rows(h_ref, gain, b_ref, row0, rows, block=16):
    half = h_ref.shape[2]
    gain_lo, gain_hi = gain[:, :half], gain[:, half:]

    def step(i, _):
        src = pl.ds(pl.multiple_of(row0 + i * block, block), block)
        dst = pl.ds(pl.multiple_of(i * block, block), block)
        lo, hi = h_ref[0, src, :].astype(F32), h_ref[1, src, :].astype(F32)
        total = jnp.sum(lo * lo, axis=-1, keepdims=True) + jnp.sum(hi * hi, axis=-1, keepdims=True)
        inv = lax.rsqrt(total / (2 * half) + EPSILON)
        b_ref[dst, :half] = (lo * inv * gain_lo).astype(BF16)
        b_ref[dst, half:] = (hi * inv * gain_hi).astype(BF16)
        return 0

    lax.fori_loop(0, rows // block, step, 0)


def rope_store(prod, cos, sin, out_ref, rows, col):
    head = cos.shape[1]
    for k in range(prod.shape[1] // head):
        vec = prod[:, k * head:(k + 1) * head].astype(BF16).astype(F32)
        rot = vec * cos + pltpu.roll(vec, head // 2, 1) * sin
        out_ref[rows, pl.ds(col + k * head, head)] = rot.astype(BF16)


def qkv_rows(b_ref, wq_ref, wk_ref, wv_ref, cos_ref, sin_ref, q_ref, k_ref, v_ref, row0, rows):
    rows_at = pl.ds(row0, rows)
    lhs = b_ref[0:rows, :]
    cos, sin = cos_ref[rows_at, :], sin_ref[rows_at, :]

    def q_tile(j, _):
        col = pl.multiple_of(j * TILE, TILE)
        prod = jnp.dot(b_ref[0:rows, :], wq_ref[:, pl.ds(col, TILE)], preferred_element_type=F32)
        rope_store(prod, cos_ref[rows_at, :], sin_ref[rows_at, :], q_ref, rows_at, col)
        return 0

    lax.fori_loop(0, wq_ref.shape[1] // TILE, q_tile, 0)
    rope_store(jnp.dot(lhs, wk_ref[...], preferred_element_type=F32), cos, sin, k_ref, rows_at, 0)
    v_ref[rows_at, :] = jnp.dot(lhs, wv_ref[...], preferred_element_type=F32).astype(BF16)


def qkv_kernel(x_hbm, gain_ref, cos_ref, sin_ref, wq_hbm, wk_hbm, wv_hbm, q_ref, k_ref, v_ref, h, b, wq, wk, wv, sems):
    half = h.shape[2]
    copies = [pltpu.make_async_copy(x_hbm.at[:, pl.ds(s * half, half)], h.at[s], sems.at[s]) for s in range(2)]
    copies += [pltpu.make_async_copy(src.at[0], dst, sems.at[2 + n]) for n, (src, dst) in enumerate(((wq_hbm, wq), (wk_hbm, wk), (wv_hbm, wv)))]
    for copy in copies:
        copy.start()
    copies[0].wait()
    copies[1].wait()
    rows = h.shape[1]
    norm_rows(h, gain_ref[...].astype(F32)[0:1, :], b, 0, rows)
    for copy in copies[2:]:
        copy.wait()
    qkv_rows(b, wq, wk, wv, cos_ref, sin_ref, q_ref, k_ref, v_ref, 0, rows)


def qkv_call(x, gain, cos, sin, w_q, w_k, w_v):
    rows, width = x.shape
    vmem = pl.BlockSpec(memory_space=pltpu.VMEM)
    hbm = pl.BlockSpec(memory_space=pl.ANY)
    return pl.pallas_call(
        qkv_kernel,
        name='qkv_first',
        out_shape=[jax.ShapeDtypeStruct((rows, w.shape[2]), BF16) for w in (w_q, w_k, w_v)],
        in_specs=[hbm, vmem, vmem, vmem, hbm, hbm, hbm],
        out_specs=[vmem] * 3,
        scratch_shapes=[
            pltpu.VMEM((2, rows, width // 2), BF16),
            pltpu.VMEM((rows, width), BF16),
            pltpu.VMEM(w_q.shape[1:], BF16),
            pltpu.VMEM(w_k.shape[1:], BF16),
            pltpu.VMEM(w_v.shape[1:], BF16),
            pltpu.SemaphoreType.DMA((5,)),
        ],
        compiler_params=pltpu.CompilerParams(vmem_limit_bytes=40 * 2**20),
    )(x, gain, cos, sin, w_q, w_k, w_v)


UNIT = 128
BATCH = 8
BITS = (8, 4, 2, 1)


def attention_kernel(layer, len_ref, q_ref, k_ref, v_ref, kc_hbm, vc_hbm, o_ref, kbuf, vbuf, qs, kf, vf, sc, od, kp, vp, sems, psems):
    rows = kc_hbm.shape[1] - 1
    seq, head = kc_hbm.shape[3], kc_hbm.shape[4]
    heads = q_ref.shape[1] // head
    kv = kc_hbm.shape[2]
    rep = heads // kv
    chunk = q_ref.shape[0] - rows
    scale = head ** -0.5
    steps = rows // BATCH

    def copies(step, slot, act):
        for i in range(BATCH):
            row = step * BATCH + i
            units = (len_ref[row] + UNIT - 1) // UNIT
            for n, bit in enumerate(BITS):
                @pl.when((units // bit) % 2 == 1)
                def _(i=i, row=row, units=units, n=n, bit=bit):
                    off = pl.multiple_of((units // (2 * bit)) * (2 * bit * UNIT), UNIT)
                    span = pl.ds(off, bit * UNIT)
                    for m, (src, dst) in enumerate(((kc_hbm, kbuf), (vc_hbm, vbuf))):
                        copy = pltpu.make_async_copy(src.at[layer, row, :, span, :], dst.at[slot, i, :, span, :], sems.at[slot, i, n, m])
                        if act == 'start':
                            copy.start()
                        else:
                            copy.wait()

    prefill = [pltpu.make_async_copy(src.at[layer, rows], dst, psems.at[n]) for n, (src, dst) in enumerate(((kc_hbm, kp), (vc_hbm, vp)))]
    for copy in prefill:
        copy.start()

    def clear(i, _):
        for slot in range(2):
            for g in range(kv):
                vbuf[slot, i, g] = jnp.zeros((seq, head), BF16)
        return 0

    lax.fori_loop(0, BATCH, clear, 0)
    copies(0, 0, 'start')

    qs[...] = jnp.zeros_like(qs)
    for h in range(heads):
        qs[h // rep, pl.ds(h, rows, stride=8), :] = q_ref[0:rows, h * head:(h + 1) * head].astype(F32)
    kf[...] = k_ref[0:rows, :].astype(F32)
    vf[...] = v_ref[0:rows, :].astype(F32)

    for copy in prefill:
        copy.wait()
    limit = len_ref[rows]

    def prefill_head(h, _):
        g = h // rep
        q = q_ref[rows:, pl.ds(pl.multiple_of(h * head, head), head)]
        kn = k_ref[rows:, pl.ds(pl.multiple_of(g * head, head), head)]
        vn = v_ref[rows:, pl.ds(pl.multiple_of(g * head, head), head)]
        dims = (((1,), (1,)), ((), ()))
        s_old = lax.dot_general(q, kp[g], dims, preferred_element_type=F32) * scale
        s_new = lax.dot_general(q, kn, dims, preferred_element_type=F32) * scale
        s_old = jnp.where(lax.broadcasted_iota(jnp.int32, s_old.shape, 1) < limit, s_old, -jnp.inf)
        causal = lax.broadcasted_iota(jnp.int32, s_new.shape, 1) <= lax.broadcasted_iota(jnp.int32, s_new.shape, 0)
        s_new = jnp.where(causal, s_new, -jnp.inf)
        top = jnp.maximum(jnp.max(s_old, axis=-1, keepdims=True), jnp.max(s_new, axis=-1, keepdims=True))
        e_old, e_new = jnp.exp(s_old - top), jnp.exp(s_new - top)
        inv = 1.0 / (jnp.sum(e_old, axis=-1, keepdims=True) + jnp.sum(e_new, axis=-1, keepdims=True))
        out = jnp.dot((e_old * inv).astype(BF16), vp[g], preferred_element_type=F32)
        out += jnp.dot((e_new * inv).astype(BF16), vn, preferred_element_type=F32)
        o_ref[rows:, pl.ds(pl.multiple_of(h * head, head), head)] = out.astype(BF16)
        return 0

    lax.fori_loop(0, heads, prefill_head, 0)

    def decode_step(step, _):
        slot = lax.rem(step, 2)

        @pl.when(step + 1 < steps)
        def _():
            copies(step + 1, 1 - slot, 'start')

        copies(step, slot, 'wait')
        for i in range(BATCH):
            row = step * BATCH + i
            length = len_ref[row]
            base = pl.multiple_of((length // 16) * 16, 16)
            hit = lax.broadcasted_iota(jnp.int32, (16, head), 0) == length - base
            for buf, new in ((kbuf, kf), (vbuf, vf)):
                for g in range(kv):
                    old = buf[slot, i, g, pl.ds(base, 16), :].astype(F32)
                    mine = new[pl.ds(pl.multiple_of(step * BATCH, BATCH), BATCH), g * head:(g + 1) * head][i:i + 1, :]
                    buf[slot, i, g, pl.ds(base, 16), :] = jnp.where(hit, mine, old).astype(BF16)
        for i in range(BATCH):
            row = step * BATCH + i
            at = pl.ds(pl.multiple_of(row * 8, 8), 8)
            q = jnp.concatenate([qs[g, at, :] for g in range(kv)], axis=-1).astype(BF16)
            keys = jnp.concatenate([kbuf[slot, i, g] for g in range(kv)], axis=-1)
            s = lax.dot_general(q, keys, (((1,), (1,)), ((), ())), preferred_element_type=F32) * scale
            s = jnp.where(lax.broadcasted_iota(jnp.int32, s.shape, 1) <= len_ref[row], s, -jnp.inf)
            sc[i * 8:(i + 1) * 8, :] = s
        for i in range(BATCH):
            s = sc[i * 8:(i + 1) * 8, :]
            e = jnp.exp(s - jnp.max(s, axis=-1, keepdims=True))
            p = (e * (1.0 / jnp.sum(e, axis=-1, keepdims=True))).astype(BF16)
            values = jnp.concatenate([vbuf[slot, i, g] for g in range(kv)], axis=-1)
            o = jnp.dot(p, values, preferred_element_type=F32)
            own = lax.broadcasted_iota(jnp.int32, (8, head), 0) // rep
            pick = o[:, 0:head]
            for g in range(1, kv):
                pick = jnp.where(own == g, o[:, g * head:(g + 1) * head], pick)
            row = step * BATCH + i
            od[pl.ds(pl.multiple_of(row * 8, 8), 8), :] = pick
        return 0

    lax.fori_loop(0, steps, decode_step, 0)
    for h in range(heads):
        o_ref[0:rows, h * head:(h + 1) * head] = od[pl.ds(h, rows, stride=8), :].astype(BF16)


def attention_call(layer, lengths, q, k, v, k_cache, v_cache):
    rows = k_cache.shape[1] - 1
    kv, seq, head = k_cache.shape[2:]
    vmem = pl.BlockSpec(memory_space=pltpu.VMEM)
    hbm = pl.BlockSpec(memory_space=pl.ANY)
    return pl.pallas_call(
        functools.partial(attention_kernel, layer),
        name=f'attention_{layer}',
        out_shape=jax.ShapeDtypeStruct(q.shape, BF16),
        in_specs=[pl.BlockSpec(memory_space=pltpu.SMEM), vmem, vmem, vmem, hbm, hbm],
        out_specs=vmem,
        scratch_shapes=[
            pltpu.VMEM((2, BATCH, kv, seq, head), BF16),
            pltpu.VMEM((2, BATCH, kv, seq, head), BF16),
            pltpu.VMEM((kv, rows * 8, head), F32),
            pltpu.VMEM((rows, kv * head), F32),
            pltpu.VMEM((rows, kv * head), F32),
            pltpu.VMEM((BATCH * 8, seq), F32),
            pltpu.VMEM((rows * 8, head), F32),
            pltpu.VMEM((kv, seq, head), BF16),
            pltpu.VMEM((kv, seq, head), BF16),
            pltpu.SemaphoreType.DMA((2, BATCH, len(BITS), 2)),
            pltpu.SemaphoreType.DMA((2,)),
        ],
        compiler_params=pltpu.CompilerParams(vmem_limit_bytes=48 * 2**20),
    )(lengths, q, k, v, k_cache, v_cache)


def block_kernel(layer, last, groups, *refs):
    if last:
        (x_hbm, att_hbm, gain_ref, wo_hbm, wg_hbm, wu_hbm, wd_hbm, out_hbm,
         xh, att, h, part, got, send, cross, b, act, wo, wg, wu, wd, lsem, osem, msem, csem, fsem) = refs
    else:
        (x_hbm, att_hbm, gain_ref, wo_hbm, wg_hbm, wu_hbm, wd_hbm, next_gain_ref, cos_ref, sin_ref, wq_hbm, wk_hbm, wv_hbm, out_hbm, q_ref, k_ref, v_ref,
         xh, att, h, part, got, send, cross, b, act, wo, wg, wu, wd, wq, wk, wv, lsem, osem, msem, csem, fsem) = refs
    tp = lax.axis_index('tp')
    core = lax.rem(tp, 2)
    mate = tp + 1 - 2 * core
    peer = lax.rem(tp + 2, 4)
    half = h.shape[2]
    own_cols = pl.ds(pl.multiple_of(core * half, half), half)

    loads = [(x_hbm.at[:, own_cols], xh), (att_hbm, att), (wo_hbm.at[layer], wo), (wg_hbm.at[layer], wg), (wu_hbm.at[layer], wu), (wd_hbm.at[layer], wd)]
    if not last:
        loads += [(wq_hbm.at[layer + 1], wq), (wk_hbm.at[layer + 1], wk), (wv_hbm.at[layer + 1], wv)]
    loads = [pltpu.make_async_copy(src, dst, lsem.at[n]) for n, (src, dst) in enumerate(loads)]
    order = [1, 2, 0, 3, 4, 5] + list(range(6, len(loads)))
    for n in order:
        loads[n].start()

    barrier = pltpu.get_barrier_semaphore()
    for other in (mate, peer):
        pl.semaphore_signal(barrier, inc=1, device_id={'tp': other}, device_id_type=MESH)
    pl.semaphore_wait(barrier, 2)

    def remote(src, dst, sem, idx, device):
        return pltpu.make_async_remote_copy(src_ref=src, dst_ref=dst, send_sem=sem.at[0, idx[0], idx[1]], recv_sem=sem.at[1, idx[0], idx[1]], device_id={'tp': device}, device_id_type=MESH)

    def to_mate(phase, g):
        at = pl.ds(*groups[g])
        return remote(part.at[1 - core, at], got.at[at], msem, (phase, g), mate)

    def to_peer(phase, g):
        at = pl.ds(*groups[g])
        return remote(send.at[at], cross.at[phase, at], csem, (phase, g), peer)

    def final(phase, g):
        at = pl.ds(*groups[g])
        return remote(h.at[core, at], h.at[core, at], fsem, (phase, g), mate)

    def project(lhs_ref, lhs_at, w_ref, g):
        row0, rows = groups[g]
        per_half = half // TILE

        def tile(j, _):
            col = pl.multiple_of(j * TILE, TILE)
            prod = jnp.dot(lhs_ref[lhs_at, :], w_ref[:, pl.ds(col, TILE)], preferred_element_type=F32)
            side = j // per_half
            part[side, pl.ds(row0, rows), pl.ds(pl.multiple_of((j - side * per_half) * TILE, TILE), TILE)] = prod.astype(BF16)
            return 0

        lax.fori_loop(0, 2 * per_half, tile, 0)

    def chip_sum(g):
        row0, rows = groups[g]

        def step(i, _):
            at = pl.ds(pl.multiple_of(row0 + i * 16, 16), 16)
            send[at, :] = (part[core, at, :].astype(F32) + got[at, :].astype(F32)).astype(BF16)
            return 0

        lax.fori_loop(0, rows // 16, step, 0)

    def add_sum(phase, base_ref, g):
        row0, rows = groups[g]

        def step(i, _):
            at = pl.ds(pl.multiple_of(row0 + i * 16, 16), 16)
            base = xh[at, :] if phase == 0 else h[core, at, :]
            total = send[at, :].astype(F32) + cross[phase, at, :].astype(F32)
            h[core, at, :] = (base.astype(F32) + total).astype(BF16)
            return 0

        lax.fori_loop(0, rows // 16, step, 0)

    loads[1].wait()
    loads[2].wait()
    for g in range(len(groups)):
        project(att, pl.ds(*groups[g]), wo, g)
        to_mate(0, g).start()
    loads[0].wait()
    for g in range(len(groups)):
        to_mate(0, g).wait()
        chip_sum(g)
        to_peer(0, g).start()
    for n in (3, 4, 5):
        loads[n].wait()
    mlp_gain = gain_ref[...].astype(F32)[layer:layer + 1, :]
    for g in range(len(groups)):
        rows = groups[g][1]
        to_peer(0, g).wait()
        add_sum(0, xh, g)
        final(0, g).start()
        final(0, g).wait()
        norm_rows(h, mlp_gain, b, groups[g][0], rows)

        def up_tile(j, _, rows=rows):
            cols = pl.ds(pl.multiple_of(j * TILE, TILE), TILE)
            gate = jnp.dot(b[0:rows, :], wg[:, cols], preferred_element_type=F32)
            up = jnp.dot(b[0:rows, :], wu[:, cols], preferred_element_type=F32)
            act[0:rows, cols] = (gate * (1.0 / (1.0 + jnp.exp(-gate))) * up).astype(BF16)
            return 0

        lax.fori_loop(0, wg.shape[1] // TILE, up_tile, 0)
        project(act, pl.ds(0, rows), wd, g)
        to_mate(1, g).start()
        to_mate(1, g).wait()
        chip_sum(g)
        to_peer(1, g).start()
    if not last:
        next_gain = next_gain_ref[...].astype(F32)[layer + 1:layer + 2, :]
        for n in (6, 7, 8):
            loads[n].wait()
    outs = []
    for g in range(len(groups)):
        row0, rows = groups[g]
        to_peer(1, g).wait()
        add_sum(1, None, g)
        final(1, g).start()
        final(1, g).wait()
        for s in range(2):
            outs.append(pltpu.make_async_copy(h.at[s, pl.ds(row0, rows)], out_hbm.at[pl.ds(row0, rows), pl.ds(s * half, half)], osem.at[g, s]))
            outs[-1].start()
        if not last:
            norm_rows(h, next_gain, b, row0, rows)
            qkv_rows(b, wq, wk, wv, cos_ref, sin_ref, q_ref, k_ref, v_ref, row0, rows)
    for copy in outs:
        copy.wait()


def block_call(layer, last, x, att, mlp_gain, w_o, w_gate, w_up, w_down, extra):
    rows, width = x.shape
    half = width // 2
    most = max(n for _, n in GROUPS)
    count = len(GROUPS)
    vmem = pl.BlockSpec(memory_space=pltpu.VMEM)
    hbm = pl.BlockSpec(memory_space=pl.ANY)
    out_shape = [jax.ShapeDtypeStruct((rows, width), BF16)]
    in_specs = [hbm, hbm, vmem, hbm, hbm, hbm, hbm]
    out_specs = [hbm]
    weights = [w_o, w_gate, w_up, w_down]
    if not last:
        in_specs += [vmem, vmem, vmem, hbm, hbm, hbm]
        weights += list(extra[3:])
        out_shape += [jax.ShapeDtypeStruct((rows, w.shape[2]), BF16) for w in extra[3:]]
        out_specs += [vmem] * 3
    return pl.pallas_call(
        functools.partial(block_kernel, layer, last, GROUPS),
        name=f'block_{layer}',
        out_shape=out_shape,
        in_specs=in_specs,
        out_specs=out_specs,
        scratch_shapes=[
            pltpu.VMEM((rows, half), BF16),
            pltpu.VMEM(att.shape, BF16),
            pltpu.VMEM((2, rows, half), BF16),
            pltpu.VMEM((2, rows, half), BF16),
            pltpu.VMEM((rows, half), BF16),
            pltpu.VMEM((rows, half), BF16),
            pltpu.VMEM((2, rows, half), BF16),
            pltpu.VMEM((most, width), BF16),
            pltpu.VMEM((most, w_down.shape[1]), BF16),
        ] + [pltpu.VMEM(w.shape[1:], BF16) for w in weights] + [
            pltpu.SemaphoreType.DMA((9,)),
            pltpu.SemaphoreType.DMA((count, 2)),
            pltpu.SemaphoreType.DMA((2, 2, count)),
            pltpu.SemaphoreType.DMA((2, 2, count)),
            pltpu.SemaphoreType.DMA((2, 2, count)),
        ],
        compiler_params=pltpu.CompilerParams(collective_id=layer, has_side_effects=True, vmem_limit_bytes=VMEM_LIMIT),
    )(x, att, mlp_gain, w_o, w_gate, w_up, w_down, *extra)


def solution(mesh):
    col_spec = P(None, None, 'tp')
    row_spec = P(None, 'tp', None)
    cache_spec = P(None, 'dp', 'tp', None, None)
    in_specs = (P('dp', None), P('dp'), P(), col_spec, col_spec, col_spec, row_spec, P(), col_spec, col_spec, row_spec, cache_spec, cache_spec)

    def body(x, lengths, attn_gain, w_q, w_k, w_v, w_o, mlp_gain, w_gate, w_up, w_down, k_cache, v_cache):
        dec_rows = lengths.shape[0] - 1
        chunk_len = x.shape[0] - dec_rows
        layers = w_q.shape[0]
        positions = jnp.concatenate([lengths[:dec_rows], lengths[dec_rows] + jnp.arange(chunk_len, dtype=jnp.int32)])
        cos, sin = rope_tables(positions, k_cache.shape[-1])
        q, k, v = qkv_call(x, attn_gain, cos, sin, w_q, w_k, w_v)
        for layer in range(layers):
            last = layer == layers - 1
            att = attention_call(layer, lengths, q, k, v, k_cache, v_cache)
            extra = () if last else (attn_gain, cos, sin, w_q, w_k, w_v)
            x, *rest = block_call(layer, last, x, att, mlp_gain, w_o, w_gate, w_up, w_down, extra)
            if not last:
                q, k, v = rest
        return x

    return jax.shard_map(body, mesh=mesh, in_specs=in_specs, out_specs=P('dp', None), check_vma=False)
```

time: 458 us -> 223 us (0.49); the launches traced: 452 us -> 223 us
  Pallas kernels: 0 us -> 206 us
  waiting for transfers between devices: 177 us -> 0 us
  matrix products: 147 us -> 0 us
  other arithmetic: 67.1 us -> 2.19 us
  local copies, waits for them, and re-layouts: 47.1 us -> 14.7 us
  between operations: 14.2 us -> 0.15 us
    pallas_call x0 -> x5, Pallas kernels: none -> 206 us  [the longest x2 141 us: block_call(): pl.pallas_call(functools.partial(block_kernel, layer, last, GROUPS), name...]
    psum x4 -> x0, waiting for transfers between devices: 177 us -> none  [the longest x2 89.4 us: decoder_layer(): attn_sum = lax.psum(attn_part, 'tp')]
    dot_general x26 -> x0, matrix products: 147 us -> none  [the longest x2 31.8 us: decoder_layer(): jnp.dot(activated, w_down, preferred_element_type=jnp.float32)]
    reduce_sum x8 -> x0, other arithmetic: 28.6 us -> none  [the longest x2 12.5 us: attention(): jax.nn.softmax(jnp.concatenate([dec_cache, dec_self], axis=-1), axis=-1)]
    convert_element_type x9 -> x1, other arithmetic: 18.3 us -> 0.73 us  [rope_tables(): positions.astype(F32)[:, None] * jnp.power(ROPE_BASE, -freq_exps)[None, :]]
    slice x13 -> x0, local copies, waits for them, and re-layouts: 14.8 us -> none  [the longest x4 11.2 us: attention(): dec_prob[..., :seq_len]]
    reduce_max x4 -> x0, other arithmetic: 11 us -> none  [the longest x2 11 us: attention(): jax.nn.softmax(jnp.concatenate([dec_cache, dec_self], axis=-1), axis=-1)]
    dot_general x2 -> x0, local copies, waits for them, and re-layouts: 10.7 us -> none  [attention(): jnp.einsum('bgrd,bgsd->bgrs', q_dec, k_cache[:dec_rows], preferred_elemen...]
  transfers between devices with their start and end apart: 4 -> 0, of which waited for: 4 -> 0; matrix products, arithmetic and copies ran while one was open for 0% -> 0% of each run, Pallas kernels for 0% -> 0%
where the time goes in v1:
time: 223 us
  Pallas kernels  206 us (92%)
  local copies, waits for them, and re-layouts  14.7 us (7%)
    pallas_call x2, Pallas kernels, block_call(): pl.pallas_call(functools.partial(block_kernel, layer, last, GROUPS), name...  141 us
    pallas_call x2, Pallas kernels, attention_call(): pl.pallas_call(functools.partial(attention_kernel, layer), name=f'attenti...  57.6 us
    unnamed x25, local copies, waits for them, and re-layouts  13.5 us
    pallas_call x1, Pallas kernels, qkv_call(): pl.pallas_call(qkv_kernel, name='qkv_first', out_shape=[jax.ShapeDtypeStr...  6.66 us

profile of v1, /device:TPU:0, one launch (start us, length us, event | category | flops | bytes accessed | tf_op | source)
XLA Modules:
  0.0 222.6 jit_solution(2120825231085117757)
XLA Ops:
  0.0 1.2 slice.7
  1.2 0.6 iota_add_fusion
  1.9 0.7 add_convert_fusion
  2.6 0.7 fusion
  3.3 0.0 copy-start.11
  3.3 0.2 pad_maximum_fusion
  3.5 0.0 copy-start.5
  3.5 0.0 copy-start.6
  3.5 0.0 copy-start
  3.5 2.0 copy-done
  5.5 0.0 copy-start.1
  5.5 1.9 copy-done.1
  7.4 0.0 copy-start.2
  7.4 1.5 copy-done.2
  8.9 0.7 copy-done.10
  9.6 6.7 %qkv_first.1 = (bf16[320,768]{1,0:T(8,128)(2,1)S(1)}, bf16[320,256]{1,0:T(8,128)(2,1)S(1)}, bf16[320,256]{1,0:T(8,128)(2,1)S(1)}) custom-call(bf16[320,3072]{1,0:T(8,128)(2,1)S(1)} %copy-done.2, bf16[2,3072]{1,0:T(2,128)(2,1)S(1)} %copy-done.10, f32[320,128]{1,0:T(8,128)S(1)} %get-tuple-element.22.cos_ref.refs_8_, ...), custom_call_target="tpu_custom_call" | custom-call | tf_op jit(solution)/shard_map/qkv_first/pallas_call | solution.py:87
  16.3 0.0 copy-done.5
  16.3 0.0 copy-done.6
  16.3 0.0 copy-done.11
  16.3 28.7 %attention_0.1.refs_1_ = bf16[320,768]{1,0:T(8,128)(2,1)S(1)} custom-call(s32[65]{0:T(128)S(1)} %copy-done.11, bf16[320,768]{1,0:T(8,128)(2,1)S(1)} %get-tuple-element.12.q_ref, bf16[320,256]{1,0:T(8,128)(2,1)S(1)} %get-tuple-element.13.k_ref, bf16[320,256]{1,0:T(8,128)(2,1)S(1)} %get-tuple-element.14.v_ref, bf16[2,65,2,1024,128]{4,3,2,1,0:T(8,128)(2,1)} %kc_hbm.3, ...), custom_call_target="tpu_custom_call" | custom-call | tf_op jit(solution)/shard_map/attention_0/pallas_call | solution.py:230
  45.0 0.0 copy-start.4
  45.1 0.8 copy-done.4
  45.8 73.0 %block_0.1 = (bf16[320,3072]{1,0:T(8,128)(2,1)}, bf16[320,768]{1,0:T(8,128)(2,1)}, bf16[320,256]{1,0:T(8,128)(2,1)}, bf16[320,256]{1,0:T(8,128)(2,1)}) custom-call(bf16[320,3072]{1,0:T(8,128)(2,1)} %refs_0_.1, bf16[320,768]{1,0:T(8,128)(2,1)} %copy-done.4, bf16[2,3072]{1,0:T(2,128)(2,1)} %refs_2_.3, bf16[2,768,3072]{2,1,0:T(8,128)(2,1)} %refs_3_.3, ...), custom_call_target="tpu_custom_call" | custom-call | tf_op jit(solution)/shard_map/block_0/pallas_call | solution.py:401
  118.8 0.0 copy-start.7
  118.8 1.0 copy-done.7
  119.9 0.9 copy-done.8
  120.8 0.9 copy-done.9
  121.7 28.9 %attention_1.1.refs_1_ = bf16[320,768]{1,0:T(8,128)(2,1)S(1)} custom-call(s32[65]{0:T(128)S(1)} %copy-done.11, bf16[320,768]{1,0:T(8,128)(2,1)S(1)} %copy-done.7, bf16[320,256]{1,0:T(8,128)(2,1)S(1)} %copy-done.8, bf16[320,256]{1,0:T(8,128)(2,1)S(1)} %copy-done.9, bf16[2,65,2,1024,128]{4,3,2,1,0:T(8,128)(2,1)} %kc_hbm.3, bf16[2,65,2,1024,128]{4,3,2,1,0:T(8,128)(2,1)} %vc_hbm.3), custom_call_target="tpu_custom_call" | custom-call | tf_op jit(solution)/shard_map/attention_1/pallas_call | solution.py:230
  150.6 0.0 copy-start.3
  150.6 0.8 copy-done.3
  151.4 68.3 %block_1.1 = bf16[320,3072]{1,0:T(8,128)(2,1)} custom-call(bf16[320,3072]{1,0:T(8,128)(2,1)} %get-tuple-element.15.refs_0_, bf16[320,768]{1,0:T(8,128)(2,1)} %copy-done.3, bf16[2,3072]{1,0:T(2,128)(2,1)} %refs_2_.3, bf16[2,768,3072]{2,1,0:T(8,128)(2,1)} %refs_3_.3, bf16[2,3072,2048]{2,1,0:T(8,128)(2,1)} %refs_4_.3, bf16[2,3072,2048]{2,1,0:T(8,128)(2,1)} %refs_5_.3, ...), custom_call_target="tpu_custom_call" | custom-call | tf_op jit(solution)/shard_map/block_1/pallas_call | solution.py:401
  219.6 2.9 %copy.15 = bf16[320,3072]{1,0:T(8,128)(2,1)} copy(bf16[320,3072]{1,0:T(8,128)(2,1)} %block_1.1) | data formatting | bytes 3932160
  (4 shorter events, 0.0 us)
Async XLA Ops:
  3.3 13.0 %copy-start.11 = (s32[65]{0:T(128)S(1)}, s32[65]{0:T(128)}, u32[]{:S(2)}) copy-start(s32[65]{0:T(128)} %len_ref.3) | copy-start | bytes 784
  3.5 12.8 %copy-start.5 = (f32[320,128]{1,0:T(8,128)}, f32[320,128]{1,0:T(8,128)S(1)}, u32[]{:S(2)}) copy-start(f32[320,128]{1,0:T(8,128)S(1)} %get-tuple-element.22.cos_ref.refs_8_) | copy-start | bytes 491524
  3.5 12.8 %copy-start.6 = (f32[320,128]{1,0:T(8,128)}, f32[320,128]{1,0:T(8,128)S(1)}, u32[]{:S(2)}) copy-start(f32[320,128]{1,0:T(8,128)S(1)} %get-tuple-element.23.sin_ref.refs_9_) | copy-start | bytes 491524
  3.5 2.0 copy-start
  5.5 1.9 copy-start.1
  7.4 1.5 copy-start.2
  8.9 0.7 copy-start.10
  45.0 0.8 copy-start.4
  118.8 1.0 copy-start.7
  119.9 0.9 copy-start.8
  120.8 0.9 copy-start.9
  150.6 0.8 copy-start.3

commit v2 on v1

--- a/solution.py
+++ b/solution.py
@@ -12,9 +12,11 @@
 MESH = pl.DeviceIdType.MESH
 F32 = jnp.float32
 BF16 = jnp.bfloat16
-VMEM_LIMIT = 66_900_000
+VMEM_LIMIT = 64_600_000
 TILE = 256
-GROUPS = ((0, 160), (160, 160))
+DOWN_TILE = 512
+SLOTS = 3
+GROUPS = ((0, 112), (112, 112), (224, 96))
 
 
 def rope_tables(positions, head_dim):
@@ -98,7 +100,7 @@
             pltpu.VMEM(w_v.shape[1:], BF16),
             pltpu.SemaphoreType.DMA((5,)),
         ],
-        compiler_params=pltpu.CompilerParams(vmem_limit_bytes=40 * 2**20),
+        compiler_params=pltpu.CompilerParams(vmem_limit_bytes=61 * 2**20),
     )(x, gain, cos, sin, w_q, w_k, w_v)
 
 
@@ -137,14 +139,15 @@
     for copy in prefill:
         copy.start()
 
-    def clear(i, _):
-        for slot in range(2):
+    for slot in range(SLOTS):
+        def clear(i, _, slot=slot):
             for g in range(kv):
                 vbuf[slot, i, g] = jnp.zeros((seq, head), BF16)
-        return 0
-
-    lax.fori_loop(0, BATCH, clear, 0)
-    copies(0, 0, 'start')
+            return 0
+
+        lax.fori_loop(0, BATCH, clear, 0)
+        if slot < SLOTS - 1:
+            copies(slot, slot, 'start')
 
     qs[...] = jnp.zeros_like(qs)
     for h in range(heads):
@@ -178,11 +181,11 @@
     lax.fori_loop(0, heads, prefill_head, 0)
 
     def decode_step(step, _):
-        slot = lax.rem(step, 2)
-
-        @pl.when(step + 1 < steps)
+        slot = lax.rem(step, SLOTS)
+
+        @pl.when(step + SLOTS - 1 < steps)
         def _():
-            copies(step + 1, 1 - slot, 'start')
+            copies(step + SLOTS - 1, lax.rem(step + SLOTS - 1, SLOTS), 'start')
 
         copies(step, slot, 'wait')
         for i in range(BATCH):
@@ -234,8 +237,8 @@
         in_specs=[pl.BlockSpec(memory_space=pltpu.SMEM), vmem, vmem, vmem, hbm, hbm],
         out_specs=vmem,
         scratch_shapes=[
-            pltpu.VMEM((2, BATCH, kv, seq, head), BF16),
-            pltpu.VMEM((2, BATCH, kv, seq, head), BF16),
+            pltpu.VMEM((SLOTS, BATCH, kv, seq, head), BF16),
+            pltpu.VMEM((SLOTS, BATCH, kv, seq, head), BF16),
             pltpu.VMEM((kv, rows * 8, head), F32),
             pltpu.VMEM((rows, kv * head), F32),
             pltpu.VMEM((rows, kv * head), F32),
@@ -243,20 +246,20 @@
             pltpu.VMEM((rows * 8, head), F32),
             pltpu.VMEM((kv, seq, head), BF16),
             pltpu.VMEM((kv, seq, head), BF16),
-            pltpu.SemaphoreType.DMA((2, BATCH, len(BITS), 2)),
+            pltpu.SemaphoreType.DMA((SLOTS, BATCH, len(BITS), 2)),
             pltpu.SemaphoreType.DMA((2,)),
         ],
-        compiler_params=pltpu.CompilerParams(vmem_limit_bytes=48 * 2**20),
+        compiler_params=pltpu.CompilerParams(vmem_limit_bytes=60 * 2**20),
     )(lengths, q, k, v, k_cache, v_cache)
 
 
 def block_kernel(layer, last, groups, *refs):
     if last:
-        (x_hbm, att_hbm, gain_ref, wo_hbm, wg_hbm, wu_hbm, wd_hbm, out_hbm,
-         xh, att, h, part, got, send, cross, b, act, wo, wg, wu, wd, lsem, osem, msem, csem, fsem) = refs
+        (x_hbm, att, gain_ref, wo_hbm, wg_hbm, wu_hbm, wd_hbm, out_hbm,
+         xh, h, part, got, send, cross, b, act, wo, wg, wu, wd, lsem, osem, msem, csem, fsem) = refs
     else:
-        (x_hbm, att_hbm, gain_ref, wo_hbm, wg_hbm, wu_hbm, wd_hbm, next_gain_ref, cos_ref, sin_ref, wq_hbm, wk_hbm, wv_hbm, out_hbm, q_ref, k_ref, v_ref,
-         xh, att, h, part, got, send, cross, b, act, wo, wg, wu, wd, wq, wk, wv, lsem, osem, msem, csem, fsem) = refs
+        (x_hbm, att, gain_ref, wo_hbm, wg_hbm, wu_hbm, wd_hbm, next_gain_ref, cos_ref, sin_ref, wq_hbm, wk_hbm, wv_hbm, out_hbm, q_ref, k_ref, v_ref,
+         xh, h, part, got, send, cross, b, act, wo, wg, wu, wd, wq, wk, wv, lsem, osem, msem, csem, fsem) = refs
     tp = lax.axis_index('tp')
     core = lax.rem(tp, 2)
     mate = tp + 1 - 2 * core
@@ -264,11 +267,11 @@
     half = h.shape[2]
     own_cols = pl.ds(pl.multiple_of(core * half, half), half)
 
-    loads = [(x_hbm.at[:, own_cols], xh), (att_hbm, att), (wo_hbm.at[layer], wo), (wg_hbm.at[layer], wg), (wu_hbm.at[layer], wu), (wd_hbm.at[layer], wd)]
+    loads = [(x_hbm.at[:, own_cols], xh), (wo_hbm.at[layer], wo), (wg_hbm.at[layer], wg), (wu_hbm.at[layer], wu), (wd_hbm.at[layer], wd)]
     if not last:
         loads += [(wq_hbm.at[layer + 1], wq), (wk_hbm.at[layer + 1], wk), (wv_hbm.at[layer + 1], wv)]
     loads = [pltpu.make_async_copy(src, dst, lsem.at[n]) for n, (src, dst) in enumerate(loads)]
-    order = [1, 2, 0, 3, 4, 5] + list(range(6, len(loads)))
+    order = [1, 0] + list(range(2, len(loads)))
     for n in order:
         loads[n].start()
 
@@ -294,16 +297,16 @@
 
     def project(lhs_ref, lhs_at, w_ref, g):
         row0, rows = groups[g]
-        per_half = half // TILE
+        per_half = half // DOWN_TILE
 
         def tile(j, _):
-            col = pl.multiple_of(j * TILE, TILE)
-            prod = jnp.dot(lhs_ref[lhs_at, :], w_ref[:, pl.ds(col, TILE)], preferred_element_type=F32)
+            col = pl.multiple_of(j * DOWN_TILE, DOWN_TILE)
+            prod = jnp.dot(lhs_ref[lhs_at, :], w_ref[:, pl.ds(col, DOWN_TILE)], preferred_element_type=F32)
             side = j // per_half
-            part[side, pl.ds(row0, rows), pl.ds(pl.multiple_of((j - side * per_half) * TILE, TILE), TILE)] = prod.astype(BF16)
+            part[side, pl.ds(row0, rows), pl.ds(pl.multiple_of((j - side * per_half) * DOWN_TILE, DOWN_TILE), DOWN_TILE)] = prod.astype(BF16)
             return 0
 
-        lax.fori_loop(0, 2 * per_half, tile, 0)
+        lax.fori_loop(0, 2 * per_half, tile, 0, unroll=2)
 
     def chip_sum(g):
         row0, rows = groups[g]
@@ -315,7 +318,7 @@
 
         lax.fori_loop(0, rows // 16, step, 0)
 
-    def add_sum(phase, base_ref, g):
+    def add_sum(phase, g):
         row0, rows = groups[g]
 
         def step(i, _):
@@ -327,26 +330,35 @@
 
         lax.fori_loop(0, rows // 16, step, 0)
 
+    count = len(groups)
+
+    def arrive(phase, g):
+        to_peer(phase, g).wait()
+        add_sum(phase, g)
+        final(phase, g).start()
+
+    def leave(phase, g):
+        to_mate(phase, g).wait()
+        chip_sum(g)
+        to_peer(phase, g).start()
+
     loads[1].wait()
-    loads[2].wait()
-    for g in range(len(groups)):
+    for g in range(count):
         project(att, pl.ds(*groups[g]), wo, g)
         to_mate(0, g).start()
+        if g > 0:
+            leave(0, g - 1)
+    leave(0, count - 1)
     loads[0].wait()
-    for g in range(len(groups)):
-        to_mate(0, g).wait()
-        chip_sum(g)
-        to_peer(0, g).start()
-    for n in (3, 4, 5):
-        loads[n].wait()
     mlp_gain = gain_ref[...].astype(F32)[layer:layer + 1, :]
-    for g in range(len(groups)):
-        rows = groups[g][1]
-        to_peer(0, g).wait()
-        add_sum(0, xh, g)
-        final(0, g).start()
+    arrive(0, 0)
+    for g in range(count):
+        row0, rows = groups[g]
         final(0, g).wait()
-        norm_rows(h, mlp_gain, b, groups[g][0], rows)
+        norm_rows(h, mlp_gain, b, row0, rows)
+        if g == 0:
+            loads[2].wait()
+            loads[3].wait()
 
         def up_tile(j, _, rows=rows):
             cols = pl.ds(pl.multiple_of(j * TILE, TILE), TILE)
@@ -355,22 +367,22 @@
             act[0:rows, cols] = (gate * (1.0 / (1.0 + jnp.exp(-gate))) * up).astype(BF16)
             return 0
 
-        lax.fori_loop(0, wg.shape[1] // TILE, up_tile, 0)
+        lax.fori_loop(0, wg.shape[1] // TILE, up_tile, 0, unroll=2)
+        if g == 0:
+            loads[4].wait()
         project(act, pl.ds(0, rows), wd, g)
         to_mate(1, g).start()
-        to_mate(1, g).wait()
-        chip_sum(g)
-        to_peer(1, g).start()
+        if g + 1 < count:
+            arrive(0, g + 1)
+        leave(1, g)
     if not last:
         next_gain = next_gain_ref[...].astype(F32)[layer + 1:layer + 2, :]
-        for n in (6, 7, 8):
+        for n in (5, 6, 7):
             loads[n].wait()
     outs = []
     for g in range(len(groups)):
         row0, rows = groups[g]
-        to_peer(1, g).wait()
-        add_sum(1, None, g)
-        final(1, g).start()
+        arrive(1, g)
         final(1, g).wait()
         for s in range(2):
             outs.append(pltpu.make_async_copy(h.at[s, pl.ds(row0, rows)], out_hbm.at[pl.ds(row0, rows), pl.ds(s * half, half)], osem.at[g, s]))
@@ -390,7 +402,7 @@
     vmem = pl.BlockSpec(memory_space=pltpu.VMEM)
     hbm = pl.BlockSpec(memory_space=pl.ANY)
     out_shape = [jax.ShapeDtypeStruct((rows, width), BF16)]
-    in_specs = [hbm, hbm, vmem, hbm, hbm, hbm, hbm]
+    in_specs = [hbm, vmem, vmem, hbm, hbm, hbm, hbm]
     out_specs = [hbm]
     weights = [w_o, w_gate, w_up, w_down]
     if not last:
@@ -406,7 +418,6 @@
         out_specs=out_specs,
         scratch_shapes=[
             pltpu.VMEM((rows, half), BF16),
-            pltpu.VMEM(att.shape, BF16),
             pltpu.VMEM((2, rows, half), BF16),
             pltpu.VMEM((2, rows, half), BF16),
             pltpu.VMEM((rows, half), BF16),
@@ -415,7 +426,7 @@
             pltpu.VMEM((most, width), BF16),
             pltpu.VMEM((most, w_down.shape[1]), BF16),
         ] + [pltpu.VMEM(w.shape[1:], BF16) for w in weights] + [
-            pltpu.SemaphoreType.DMA((9,)),
+            pltpu.SemaphoreType.DMA((8,)),
             pltpu.SemaphoreType.DMA((count, 2)),
             pltpu.SemaphoreType.DMA((2, 2, count)),
             pltpu.SemaphoreType.DMA((2, 2, count)),

time: 223 us -> 201 us (0.901)
  Pallas kernels: 206 us -> 193 us
  local copies, waits for them, and re-layouts: 14.7 us -> 4.18 us
    pallas_call x2, Pallas kernels: 141 us -> 121 us  [block_call(): pl.pallas_call(functools.partial(block_kernel, layer, last, GROUPS), name...]
    unnamed x25 -> x1, local copies, waits for them, and re-layouts: 13.5 us -> 2.94 us
    pallas_call x2, Pallas kernels: 57.6 us -> 62.6 us  [attention_call(): pl.pallas_call(functools.partial(attention_kernel, layer), name=f'attenti...]
    pallas_call x1, Pallas kernels: 6.66 us -> 9.41 us  [qkv_call(): pl.pallas_call(qkv_kernel, name='qkv_first', out_shape=[jax.ShapeDtypeStr...]
where the time goes in v2:
time: 201 us; the launch traced here: 200 us
  Pallas kernels  193 us (96%)
  local copies, waits for them, and re-layouts  4.18 us (2%)
  other arithmetic  2.94 us (1%)
    pallas_call x2, Pallas kernels, block_call(): pl.pallas_call(functools.partial(block_kernel, layer, last, GROUPS), name...  121 us
    pallas_call x2, Pallas kernels, attention_call(): pl.pallas_call(functools.partial(attention_kernel, layer), name=f'attenti...  62.6 us
    pallas_call x1, Pallas kernels, qkv_call(): pl.pallas_call(qkv_kernel, name='qkv_first', out_shape=[jax.ShapeDtypeStr...  9.41 us

profile of v2, /device:TPU:0, one launch (start us, length us, event | category | flops | bytes accessed | tf_op | source)
XLA Modules:
  0.0 200.4 jit_solution(3002045775984417471)
XLA Ops:
  0.0 1.2 slice.7
  1.2 0.6 iota_add_fusion
  1.9 0.7 add_convert_fusion
  2.6 0.7 fusion
  3.3 0.9 pad_maximum_fusion
  4.2 9.4 %qkv_first.1 = (bf16[320,768]{1,0:T(8,128)(2,1)}, bf16[320,256]{1,0:T(8,128)(2,1)}, bf16[320,256]{1,0:T(8,128)(2,1)}) custom-call(bf16[320,3072]{1,0:T(8,128)(2,1)} %refs_0_.1, bf16[2,3072]{1,0:T(2,128)(2,1)} %refs_7_.1, f32[320,128]{1,0:T(8,128)} %get-tuple-element.22.cos_ref.refs_8_, f32[320,128]{1,0:T(8,128)} %get-tuple-element.23.sin_ref.refs_9_, ...), custom_call_target="tpu_custom_call" | custom-call | tf_op jit(solution)/shard_map/qkv_first/pallas_call | solution.py:89
  13.6 31.3 %attention_0.1.refs_1_ = bf16[320,768]{1,0:T(8,128)(2,1)} custom-call(s32[65]{0:T(128)} %len_ref.3, bf16[320,768]{1,0:T(8,128)(2,1)} %get-tuple-element.12.q_ref, bf16[320,256]{1,0:T(8,128)(2,1)} %get-tuple-element.13.k_ref, bf16[320,256]{1,0:T(8,128)(2,1)} %get-tuple-element.14.v_ref, bf16[2,65,2,1024,128]{4,3,2,1,0:T(8,128)(2,1)} %kc_hbm.3, ...), custom_call_target="tpu_custom_call" | custom-call | tf_op jit(solution)/shard_map/attention_0/pallas_call | solution.py:233
  44.9 63.7 %block_0.1 = (bf16[320,3072]{1,0:T(8,128)(2,1)}, bf16[320,768]{1,0:T(8,128)(2,1)}, bf16[320,256]{1,0:T(8,128)(2,1)}, bf16[320,256]{1,0:T(8,128)(2,1)}) custom-call(bf16[320,3072]{1,0:T(8,128)(2,1)} %refs_0_.1, bf16[320,768]{1,0:T(8,128)(2,1)} %attention_0.1.refs_1_, bf16[2,3072]{1,0:T(2,128)(2,1)} %refs_2_.3, bf16[2,768,3072]{2,1,0:T(8,128)(2,1)} %refs_3_.3, ...), custom_call_target="tpu_custom_call" | custom-call | tf_op jit(solution)/shard_map/block_0/pallas_call | solution.py:413
  108.7 31.3 %attention_1.1.refs_1_ = bf16[320,768]{1,0:T(8,128)(2,1)} custom-call(s32[65]{0:T(128)} %len_ref.3, bf16[320,768]{1,0:T(8,128)(2,1)} %get-tuple-element.16.q_ref, bf16[320,256]{1,0:T(8,128)(2,1)} %get-tuple-element.17.k_ref, bf16[320,256]{1,0:T(8,128)(2,1)} %get-tuple-element.18.v_ref, bf16[2,65,2,1024,128]{4,3,2,1,0:T(8,128)(2,1)} %kc_hbm.3, ...), custom_call_target="tpu_custom_call" | custom-call | tf_op jit(solution)/shard_map/attention_1/pallas_call | solution.py:233
  139.9 57.5 %block_1.1 = bf16[320,3072]{1,0:T(8,128)(2,1)} custom-call(bf16[320,3072]{1,0:T(8,128)(2,1)} %get-tuple-element.15.refs_0_, bf16[320,768]{1,0:T(8,128)(2,1)} %attention_1.1.refs_1_, bf16[2,3072]{1,0:T(2,128)(2,1)} %refs_2_.3, bf16[2,768,3072]{2,1,0:T(8,128)(2,1)} %refs_3_.3, bf16[2,3072,2048]{2,1,0:T(8,128)(2,1)} %refs_4_.3, bf16[2,3072,2048]{2,1,0:T(8,128)(2,1)} %refs_5_.3, ...), custom_call_target="tpu_custom_call" | custom-call | tf_op jit(solution)/shard_map/block_1/pallas_call | solution.py:413
  197.5 2.9 %copy.15 = bf16[320,3072]{1,0:T(8,128)(2,1)} copy(bf16[320,3072]{1,0:T(8,128)(2,1)} %block_1.1) | data formatting | bytes 3932160
  (1 shorter events, 0.0 us)
